TPU v7x, 256 devices: a whole 4x4x8 slice. The times are simulated.
256 devices in a mesh: ent: 8 (over x, core), blk: 4 (over y), rel: 8 (over z).
Axes of the slice: x: 4, y: 4, z: 8, core: 2. Of those that a mesh axis runs over, the one named last changes fastest.
Arguments:
- factors: bfloat16 [32768, 256], P(('ent', 'blk')), may hold values from -12 to 12
- heads: int32 [32, 8, 1, 32768], P(None, 'rel', None, ('ent', 'blk')), may hold values from 0 to 1023, as said below
- tails: int32 [32, 8, 1, 32768], P(None, 'rel', None, ('ent', 'blk')), may hold values from 0 to 1023, as said below
- values: float32 [32, 8, 1, 32768], P(None, 'rel', None, ('ent', 'blk')), may hold values from 0.3 to 9
Outputs:
- relation_fit: float32 [256, 256, 256], P(('ent', 'blk', 'rel'))
- residual: float32 [256, 256, 256], P(('ent', 'blk', 'rel'))
Inputs may be any that keep to these rules, and one draw needn't show every extreme that they name: In every aligned tile of 128 triple columns (columns 128 t to 128 t + 127 of one relation) all heads lie in one aligned block of 128 positions (128 b to 128 b + 127). In every aligned tile of 128 triple columns all tails lie in one aligned block of 128 positions.
All inputs are finite; a program needn't handle non-finite values.
Results may differ from a plain program's by a relative error of at most 0.0029.
Values sent between devices are 32-bit elements; how exact they have to be, the bound alone decides.
No kernel may reach another device: no remote copies, remote signals or barrier semaphores. Data moves between devices by JAX's collectives and lax.ppermute only.
A program may use at most 128 MiB of HBM per device.

v0:
```python
import functools
import math

import jax
import jax.numpy as jnp
from jax import lax
from jax.experimental import pallas as pl
from jax.experimental.pallas import tpu as pltpu
from jax.sharding import Mesh
from jax.sharding import PartitionSpec as P

F32 = jnp.float32
BF16 = jnp.bfloat16
ITERS = 8
TILE = 128
RIDGE = 0.01
TINY = 1e-12
ENT_BLK_REL = ("ent_0", "ent_1", "blk", "rel")
ENT_BLK = ("ent_0", "ent_1", "blk")
BASIS = ITERS + 1
PAIRS = [(i, j) for j in range(BASIS) for i in range(j + 1)]
PAIR_ROWS = -(-len(PAIRS) // 8) * 8


def tables_kernel(
    factors_hbm, heads_hbm, tails_hbm, values_hbm, table_ref, gram_ref, heads_ref, tails_ref, values_ref, factors_ref, sems
):
    sources = (factors_hbm, heads_hbm, tails_hbm, values_hbm)
    targets = (factors_ref, heads_ref, tails_ref, values_ref)
    copies = [pltpu.make_async_copy(s, t, sems.at[k]) for k, (s, t) in enumerate(zip(sources, targets))]
    for copy in copies:
        copy.start()
    copies[0].wait()
    gram = None
    for b in range(factors_ref.shape[0] // TILE):
        rows = factors_ref[b * TILE : (b + 1) * TILE, :]
        columns = rows.astype(F32).T
        table_ref[b] = columns
        part = jnp.dot(columns.astype(BF16), rows, preferred_element_type=F32)
        gram = part if gram is None else gram + part
    half = gram.shape[0] // 2
    gram_ref[:half] = gram[:half, :half]
    gram_ref[half : 2 * half] = gram[:half, half:]
    gram_ref[2 * half :] = gram[half:, half:]
    for copy in copies[1:]:
        copy.wait()


def resident(*arrays):
    return tuple(pltpu.with_memory_space_constraint(a, pltpu.VMEM) for a in arrays)


LEAN = pltpu.CompilerParams(vmem_limit_bytes=16 * 2**20)


def cost(products, moved=0):
    return pl.CostEstimate(flops=products * 2 * 256**3, bytes_accessed=moved, transcendentals=0)


IN_VMEM = pl.BlockSpec(memory_space=pltpu.VMEM)
IN_SMEM = pl.BlockSpec(memory_space=pltpu.SMEM)


def tables(factors, heads, tails, values):
    ents, rank = factors.shape
    return pl.pallas_call(
        tables_kernel,
        in_specs=[pl.BlockSpec(memory_space=pltpu.HBM)] * 4,
        out_shape=(
            pltpu.VMEM((ents // TILE, rank, TILE), F32),
            pltpu.VMEM((3 * rank // 2, rank // 2), F32),
            pltpu.VMEM(heads.shape, jnp.int32),
            pltpu.VMEM(tails.shape, jnp.int32),
            pltpu.VMEM(values.shape, F32),
        ),
        scratch_shapes=[pltpu.VMEM(factors.shape, BF16), pltpu.SemaphoreType.DMA((4,))],
        compiler_params=LEAN,
        name="tables",
    )(*(pltpu.with_memory_space_constraint(a, pltpu.HBM) for a in (factors, heads, tails, values)))


def square_of(packed, ents):
    half = packed.shape[1]
    packed = packed * (1.0 / ents)
    corner = packed[half : 2 * half]
    upper = jnp.concatenate([packed[:half], corner], axis=1)
    lower = jnp.concatenate([corner.T, packed[2 * half :]], axis=1)
    return jnp.concatenate([upper, lower], axis=0)


def lane_pick(block, ids):
    dims = lax.GatherDimensionNumbers(
        offset_dims=(),
        collapsed_slice_dims=(1,),
        start_index_map=(1,),
        operand_batching_dims=(0,),
        start_indices_batching_dims=(0,),
    )
    return lax.gather(
        block, ids[..., None], dims, (1, 1), mode=lax.GatherScatterMode.PROMISE_IN_BOUNDS
    )


def triple_kernel(heads_ref, tails_ref, values_ref, table_ref, *rest, first, scale, halves):
    if halves:
        partner_ref, upper_ref, lower_ref = rest[-3:]
    else:
        out_ref = rest[-1]
    rank = table_ref.shape[1]
    width = heads_ref.shape[2]
    x, core, y = (lax.axis_index(a) for a in ENT_BLK)
    to_core = core if halves else 1 - core
    columns = lax.axis_size("blk")

    def rows(ids_ref, relation, tile):
        at = slice(tile * TILE, (tile + 1) * TILE)
        block = ids_ref[relation, 0, tile * TILE] // TILE
        inside = jnp.broadcast_to(ids_ref[relation, :, at] & (TILE - 1), (rank, TILE))
        return lane_pick(table_ref[block], inside).astype(BF16)

    for i in range(columns):
        to_x = x ^ jnp.where(to_core == 0, first, i)
        to_y = y ^ jnp.where(to_core == 0, i, first)
        relation = (to_x * 2 + to_core) * columns + to_y
        summed = None
        for pair in range(0, width // TILE, 2):
            tiles = range(pair, min(pair + 2, width // TILE))
            weighted = []
            for tile in tiles:
                at = slice(tile * TILE, (tile + 1) * TILE)
                head_rows = rows(heads_ref, relation, tile).astype(F32)
                weighted.append((head_rows * values_ref[relation, :, at]).astype(BF16))
            weighted = jnp.concatenate(weighted, axis=1)
            tail_rows = jnp.concatenate([rows(tails_ref, relation, tile) for tile in tiles], axis=1)
            part = lax.dot_general(
                weighted, tail_rows, (((1,), (1,)), ((), ())), preferred_element_type=F32
            )
            summed = part if summed is None else summed + part
        summed = summed * scale
        if halves:
            summed = summed + partner_ref[i]
            upper_ref[i] = summed[: rank // 2]
            lower_ref[i] = summed[rank // 2 :]
        else:
            out_ref[i] = summed


def triple_sums(first, heads, tails, values, table, scale, partner=None, after=None):
    count = lax.axis_size("blk")
    width = heads.shape[2]
    rank = table.shape[1]
    args = [heads, tails, values, table]
    if after is not None:
        args.append(after)
    if partner is None:
        shape = pltpu.VMEM((count, rank, rank), F32)
    else:
        args.append(partner)
        shape = (pltpu.VMEM((count, rank // 2, rank), F32),) * 2
    return pl.pallas_call(
        functools.partial(triple_kernel, first=first, scale=scale, halves=partner is not None),
        in_specs=[IN_VMEM] * len(args),
        out_shape=shape,
        compiler_params=LEAN,
        cost_estimate=cost(count * width // 256),
    )(*resident(*args))


def total(array):
    return jnp.sum(jnp.sum(array, axis=0, keepdims=True), axis=1, keepdims=True)


def split(array):
    high = array.astype(BF16)
    return high, (array - high.astype(F32)).astype(BF16)


def dot(a, b):
    return jnp.dot(a, b, preferred_element_type=F32)


def signs(rank):
    i = lax.broadcasted_iota(jnp.int32, (rank, rank), 0)
    j = lax.broadcasted_iota(jnp.int32, (rank, rank), 1)
    mixed = i * 40503 + j * 30011 + 12345
    for step in (7, 3):
        mixed = mixed ^ lax.shift_right_logical(mixed, jnp.full_like(mixed, step * 2))
        mixed = mixed * 739982445
    mixed = mixed ^ lax.shift_right_logical(mixed, jnp.full_like(mixed, 15))
    return jnp.where((mixed & 64) == 0, 1.0, -1.0).astype(F32)


def basis_kernel(gram_ref, ua_ref, ub_ref, la_ref, lb_ref, basis_ref, inner_ref, coef_ref, sums_ref, *, ents):
    gram = square_of(gram_ref[...], ents)
    rank = gram.shape[0]
    half = rank // 2
    basis_ref[0, :half, :] = ua_ref[...] + ub_ref[...]
    basis_ref[0, half:, :] = la_ref[...] + lb_ref[...]
    sums_ref[...] = jnp.zeros_like(sums_ref)
    norm2 = total(gram * gram)
    inverse = lax.rsqrt(norm2)
    g_high, g_low = split(gram * inverse)

    def rough(v):
        return dot(g_high, dot(v.astype(BF16), g_high).astype(BF16))

    def put(row, value):
        coef_ref[row : row + 1, :] = jnp.broadcast_to(value, (1, rank))

    put(0, norm2)
    now = signs(rank)
    ahead = rough(now)
    size = lax.rsqrt(jnp.maximum(total(now * ahead), TINY))
    now = now * size
    ahead = ahead * size
    before = None
    behind = None
    off = None
    row = 0
    for step in range(BASIS):
        vector = basis_ref[step]
        if step < ITERS:
            v_high, v_low = split(vector)
            right = dot(v_high, g_high) + (dot(v_low, g_high) + dot(v_high, g_low))
            next_image = rough(ahead)
            r_high, r_low = split(right)
            image = dot(g_high, r_high) + (dot(g_low, r_high) + dot(g_high, r_low))
            diagonal = total(ahead * ahead)
            rest = ahead - diagonal * now
            rest_image = next_image - diagonal * ahead
            image = image - diagonal * vector
            if step:
                rest = rest - off * before
                rest_image = rest_image - off * behind
                image = image - off * basis_ref[step - 1]
            square = jnp.maximum(total(rest * rest_image), TINY)
            inverse_off = lax.rsqrt(square)
            off = square * inverse_off
            put(1 + step, diagonal)
            put(1 + ITERS + step, off)
            basis_ref[step + 1] = image * inverse_off
            before = now
            behind = ahead
            now = rest * inverse_off
            ahead = rest_image * inverse_off
        for other in range(step + 1):
            product = jnp.sum(basis_ref[other] * vector, axis=0, keepdims=True)
            sums_ref[row : row + 1, :] = product[:, :TILE] + product[:, TILE:]
            row += 1
    ones = jnp.ones((TILE, TILE), F32)
    spread = jnp.dot(sums_ref[...], ones, preferred_element_type=F32, precision=lax.Precision.HIGHEST)
    r = lax.broadcasted_iota(jnp.int32, spread.shape, 0)
    c = lax.broadcasted_iota(jnp.int32, spread.shape, 1)
    packed = jnp.sum(jnp.where(r == c, spread, 0.0), axis=0, keepdims=True)
    inner_ref[...] = jnp.broadcast_to(packed[None], inner_ref.shape)


COEF_ROWS = -(-(1 + 2 * ITERS) // 8) * 8


def basis_of(gram, parts, devices, ents):
    rank = 2 * gram.shape[1]
    return pl.pallas_call(
        functools.partial(basis_kernel, ents=ents),
        out_shape=(
            pltpu.VMEM((BASIS, rank, rank), F32),
            pltpu.VMEM((devices, 1, TILE), F32),
            pltpu.VMEM((COEF_ROWS, rank), F32),
        ),
        in_specs=[IN_VMEM] * (1 + len(parts)),
        scratch_shapes=[pltpu.VMEM((PAIR_ROWS, TILE), F32)],
        compiler_params=LEAN,
        cost_estimate=cost(8 * ITERS),
        name="basis",
    )(*resident(gram, *parts))


def tree(terms):
    terms = list(terms)
    while len(terms) > 1:
        terms = [sum(terms[i : i + 2][1:], terms[i]) for i in range(0, len(terms), 2)]
    return terms[0]


def solve_kernel(inner_ref, coef_ref, basis_ref, fit_ref, residual_ref, spread_ref):
    rank = basis_ref.shape[1]
    summed = jnp.sum(inner_ref[:, 0, :], axis=0, keepdims=True)
    r = lax.broadcasted_iota(jnp.int32, spread_ref.shape, 0)
    c = lax.broadcasted_iota(jnp.int32, spread_ref.shape, 1)
    alone = jnp.where(r == c, jnp.broadcast_to(summed, spread_ref.shape), 0.0)
    ones = jnp.ones((TILE, TILE), F32)
    spread_ref[...] = jnp.dot(alone, ones, preferred_element_type=F32, precision=lax.Precision.HIGHEST)

    def whole(value):
        return jnp.broadcast_to(value, (8, TILE))

    inner = {}
    for k, (i, j) in enumerate(PAIRS):
        inner[i, j] = inner[j, i] = whole(spread_ref[k : k + 1, :])
    norm2 = whole(coef_ref[0:1, :TILE])
    diagonal = [whole(coef_ref[1 + k : 2 + k, :TILE]) for k in range(ITERS)]
    off = [whole(coef_ref[1 + ITERS + k : 2 + ITERS + k, :TILE]) for k in range(ITERS)]

    def image(v):
        out = []
        for k in range(len(v) + 1):
            terms = []
            if k < len(v):
                terms.append(diagonal[k] * v[k])
            if k > 0:
                terms.append(off[k - 1] * v[k - 1])
            if k + 1 < len(v):
                terms.append(off[k] * v[k + 1])
            value = norm2 * tree(terms)
            out.append(value + RIDGE * v[k] if k < len(v) else value)
        return out

    def product(u, v):
        return tree([u[i] * tree([inner[i, j] * v[j] for j in range(len(v))]) for i in range(len(u))])

    one = jnp.ones((8, TILE), F32)
    residual = [one]
    direction = [one]
    fit = None
    norm_now = inner[0, 0]
    for step in range(ITERS):
        along = image(direction)
        size = norm_now / product(direction, along)
        if fit is None:
            fit = [size * direction[0]]
        else:
            fit = [f + size * d for f, d in zip(fit, direction)] + [size * direction[-1]]
        residual = [p - size * q for p, q in zip(residual, along)] + [-size * along[-1]]
        if step + 1 < ITERS:
            norm_next = product(residual, residual)
            ratio = norm_next / norm_now
            direction = [p + ratio * d for p, d in zip(residual, direction)] + [residual[-1]]
            norm_now = norm_next

    def lanes(value):
        return jnp.concatenate([value[0:1, :]] * (rank // TILE), axis=1)

    fit = [lanes(v) for v in fit]
    residual = [lanes(v) for v in residual]
    for top in range(0, rank, 32):
        at = slice(top, top + 32)
        parts = [basis_ref[k, at, :] for k in range(BASIS)]
        fit_ref[0, at, :] = tree([fit[k] * parts[k] for k in range(ITERS)])
        residual_ref[0, at, :] = tree([residual[k] * parts[k] for k in range(BASIS)])


def solve(inner, coef, basis):
    rank = basis.shape[1]
    return pl.pallas_call(
        solve_kernel,
        out_shape=(jax.ShapeDtypeStruct((1, rank, rank), F32),) * 2,
        in_specs=[IN_VMEM] * 3,
        scratch_shapes=[pltpu.VMEM((PAIR_ROWS, TILE), F32)],
        compiler_params=LEAN,
        name="solve",
    )(*resident(inner, coef, basis))


def shifted(array, bit):
    axes = ENT_BLK
    sizes = [lax.axis_size(a) for a in axes]
    pairs = []
    for x in range(sizes[0]):
        for core in range(sizes[1]):
            for y in range(sizes[2]):
                to = [x, core, y]
                if bit == "core":
                    to[1] ^= 1
                else:
                    near = bit[0] == "1"
                    axis = 0 if near == (core == 0) else 2
                    to[axis] ^= 1 if bit[1] == "e" else 3
                pairs.append(
                    ((x * sizes[1] + core) * sizes[2] + y, (to[0] * sizes[1] + to[1]) * sizes[2] + to[2])
                )
    return lax.ppermute(array, axes, pairs)


def fit(factors, heads, tails, values):
    shards = lax.axis_size(ENT_BLK)
    ent_dev = factors.shape[0]
    width = heads.shape[3]
    relations = heads.shape[0] * heads.shape[2]
    scale = 1.0 / math.sqrt(shards * width)
    heads = heads.reshape(relations, 1, width)
    tails = tails.reshape(relations, 1, width)
    values = values.reshape(relations, 1, width)
    ents = ent_dev * shards
    table, gram_part, heads, tails, values = tables(factors, heads, tails, values)
    gram = gram_part
    for bit in ("core", "1e", "1o", "2e", "2o"):
        gram = gram + shifted(gram, bit)
    sums = functools.partial(
        triple_sums, heads=heads, tails=tails, values=values, table=table, scale=scale
    )
    upper, lower = {}, {}
    from_partner = {}

    def give(first, after=None):
        partial = sums(first, after=after)
        from_partner[first] = shifted(partial, "core")
        return partial

    def keep(first, after=None):
        upper[first], lower[first] = sums(first, partner=from_partner[first], after=after)

    give(2)
    give(1)
    keep(2)
    third = give(3, upper[2])
    keep(1, third)
    keep(3, upper[1])
    give(0, upper[3])
    keep(0)

    up2 = shifted(upper[2], "1e")
    low2 = shifted(lower[2], "1o")
    up1 = shifted(upper[1], "1e")
    low3 = shifted(lower[3], "1o")
    up_b = shifted(upper[3] + up2, "1o")
    low_b = shifted(lower[1] + low2, "1e")
    up_c = upper[0][1:3] + up1[1:3] + up_b[1:3]
    low_c = lower[0][2:4] + low3[2:4] + low_b[2:4]
    up_c = shifted(up_c, "2e")
    low_c = shifted(low_c, "2o")
    up_d = shifted(upper[0][3] + up1[3] + up_b[3] + up_c[1], "2o")
    low_d = shifted(lower[0][1] + low3[1] + low_b[1] + low_c[0], "2e")
    up_own = upper[0][0] + up1[0] + up_b[0] + up_c[0]
    low_own = lower[0][0] + low3[0] + low_b[0] + low_c[1]

    devices = lax.axis_size(ENT_BLK_REL)
    basis, inner, coef = basis_of(gram, (up_own, up_d, low_own, low_d), devices, ents)
    inner = lax.all_to_all(inner, ENT_BLK_REL, 0, 0, tiled=True)
    return solve(inner, coef, basis)


def solution(mesh):
    torus = Mesh(
        mesh.devices.reshape(mesh.shape["ent"] // 2, 2, mesh.shape["blk"], mesh.shape["rel"]),
        ENT_BLK_REL,
    )
    spread = P(None, "rel", None, ENT_BLK)
    whole = P(ENT_BLK_REL, None, None)
    return jax.shard_map(
        fit,
        mesh=torus,
        in_specs=(P(ENT_BLK, None), spread, spread, spread),
        out_specs=(whole, whole),
        check_vma=False,
    )
```

profile of v0, /device:TPU:1, one launch (start us, length us, event | category | flops | bytes accessed | tf_op | source)
XLA Modules:
  0.0 103.8 jit_solution(1571455544757455792)
XLA Ops:
  0.6 1.6 %tables.1 = (f32[8,256,128]{2,1,0:T(8,128)S(1)}, f32[384,128]{1,0:T(8,128)S(1)}, s32[32,1,1024]{2,1,0:T(1,128)S(1)}, s32[32,1,1024]{2,1,0:T(1,128)S(1)}, f32[32,1,1024]{2,1,0:T(1,128)S(1)}) custom-call(bf16[1024,256]{1,0:T(8,128)(2,1)} %factors_hbm.1, s32[32,1,1024]{2,1,0:T(1,128)} %bitcast.11, s32[32,1,1024]{2,1,0:T(1,128)} %bitcast.12, f32[32,1,1024]{2,1,0:T(1,128)} %bitcast.13), custom_call_target="tpu_custom_call" | custom-call | tf_op jit(solution)/shard_map/tables/pallas_call | solution.py:66
  2.2 1.8 %shard_map.59 = f32[4,256,256]{2,1,0:T(8,128)S(1)} custom-call(s32[32,1,1024]{2,1,0:T(1,128)S(1)} %get-tuple-element.19.heads_ref, s32[32,1,1024]{2,1,0:T(1,128)S(1)} %get-tuple-element.20.tails_ref, f32[32,1,1024]{2,1,0:T(1,128)S(1)} %get-tuple-element.21.values_ref, f32[8,256,128]{2,1,0:T(8,128)S(1)} %get-tuple-element.22.table_ref), custom_call_target="tpu_custom_call" | custom-call | flops 536870912 | tf_op jit(solution)/shard_map/pallas_call | solution.py:160
  4.0 3.3 %collective-permute-start.5 = (f32[4,256,256]{2,1,0:T(8,128)S(1)}, f32[4,256,256]{2,1,0:T(8,128)S(1)}, u32[]{:S(2)}, u32[]{:S(2)}) collective-permute-start(f32[4,256,256]{2,1,0:T(8,128)S(1)} %shard_map.59), channel_id=1, source_target_pairs={{0,32},{8,40},{16,48},{24,56},{32,0},{40,8},{48,16},{56,24},{64,96... | collective-permute-start | bytes 3145736 | tf_op jit(solution)/shard_map/ppermute | solution.py:381
  7.3 1.8 %shard_map.62 = f32[4,256,256]{2,1,0:T(8,128)S(1)} custom-call(s32[32,1,1024]{2,1,0:T(1,128)S(1)} %get-tuple-element.19.heads_ref, s32[32,1,1024]{2,1,0:T(1,128)S(1)} %get-tuple-element.20.tails_ref, f32[32,1,1024]{2,1,0:T(1,128)S(1)} %get-tuple-element.21.values_ref, f32[8,256,128]{2,1,0:T(8,128)S(1)} %get-tuple-element.22.table_ref), custom_call_target="tpu_custom_call" | custom-call | flops 536870912 | tf_op jit(solution)/shard_map/pallas_call | solution.py:160
  9.6 1.8 %shard_map.60 = (f32[4,128,256]{2,1,0:T(8,128)S(1)}, f32[4,128,256]{2,1,0:T(8,128)S(1)}) custom-call(s32[32,1,1024]{2,1,0:T(1,128)S(1)} %get-tuple-element.19.heads_ref, s32[32,1,1024]{2,1,0:T(1,128)S(1)} %get-tuple-element.20.tails_ref, f32[32,1,1024]{2,1,0:T(1,128)S(1)} %get-tuple-element.21.values_ref, f32[8,256,128]{2,1,0:T(8,128)S(1)} %get-tuple-element.22.table_ref, ...), custom_call_target="tpu_custom_call" | custom-call | flops 536870912 | tf_op jit(solution)/shard_map/pallas_call | solution.py:160
  11.5 1.8 %shard_map.61.rest_0_ = f32[4,256,256]{2,1,0:T(8,128)S(1)} custom-call(s32[32,1,1024]{2,1,0:T(1,128)S(1)} %get-tuple-element.19.heads_ref, s32[32,1,1024]{2,1,0:T(1,128)S(1)} %get-tuple-element.20.tails_ref, f32[32,1,1024]{2,1,0:T(1,128)S(1)} %get-tuple-element.21.values_ref, f32[8,256,128]{2,1,0:T(8,128)S(1)} %get-tuple-element.22.table_ref, ...), custom_call_target="tpu_custom_call" | custom-call | flops 536870912 | tf_op jit(solution)/shard_map/pallas_call | solution.py:160
  13.9 1.8 %shard_map.63 = (f32[4,128,256]{2,1,0:T(8,128)S(1)}, f32[4,128,256]{2,1,0:T(8,128)S(1)}) custom-call(s32[32,1,1024]{2,1,0:T(1,128)S(1)} %get-tuple-element.19.heads_ref, s32[32,1,1024]{2,1,0:T(1,128)S(1)} %get-tuple-element.20.tails_ref, f32[32,1,1024]{2,1,0:T(1,128)S(1)} %get-tuple-element.21.values_ref, f32[8,256,128]{2,1,0:T(8,128)S(1)} %get-tuple-element.22.table_ref, ...), custom_call_target="tpu_custom_call" | custom-call | flops 536870912 | tf_op jit(solution)/shard_map/pallas_call | solution.py:160
  16.2 1.8 %shard_map.64 = (f32[4,128,256]{2,1,0:T(8,128)S(1)}, f32[4,128,256]{2,1,0:T(8,128)S(1)}) custom-call(s32[32,1,1024]{2,1,0:T(1,128)S(1)} %get-tuple-element.19.heads_ref, s32[32,1,1024]{2,1,0:T(1,128)S(1)} %get-tuple-element.20.tails_ref, f32[32,1,1024]{2,1,0:T(1,128)S(1)} %get-tuple-element.21.values_ref, f32[8,256,128]{2,1,0:T(8,128)S(1)} %get-tuple-element.22.table_ref, ...), custom_call_target="tpu_custom_call" | custom-call | flops 536870912 | tf_op jit(solution)/shard_map/pallas_call | solution.py:160
  18.1 1.8 %shard_map.65 = f32[4,256,256]{2,1,0:T(8,128)S(1)} custom-call(s32[32,1,1024]{2,1,0:T(1,128)S(1)} %get-tuple-element.19.heads_ref, s32[32,1,1024]{2,1,0:T(1,128)S(1)} %get-tuple-element.20.tails_ref, f32[32,1,1024]{2,1,0:T(1,128)S(1)} %get-tuple-element.21.values_ref, f32[8,256,128]{2,1,0:T(8,128)S(1)} %get-tuple-element.22.table_ref, ...), custom_call_target="tpu_custom_call" | custom-call | flops 536870912 | tf_op jit(solution)/shard_map/pallas_call | solution.py:160
  21.6 1.3 %collective-permute-start.10 = (f32[4,128,256]{2,1,0:T(8,128)S(1)}, f32[4,128,256]{2,1,0:T(8,128)S(1)}, u32[]{:S(2)}, u32[]{:S(2)}) collective-permute-start(f32[4,128,256]{2,1,0:T(8,128)S(1)} %get-tuple-element.23.rest_0_), channel_id=1, source_target_pairs={{0,64},{8,72},{16,80},{24,88},{32,40},{40,32},{48,56},{56,48},{64,... | collective-permute-start | bytes 1572872 | tf_op jit(solution)/shard_map/ppermute | solution.py:381
  23.0 1.1 %collective-permute-start.1 = (f32[384,128]{1,0:T(8,128)S(1)}, f32[384,128]{1,0:T(8,128)S(1)}, u32[]{:S(2)}, u32[]{:S(2)}) collective-permute-start(f32[384,128]{1,0:T(8,128)S(1)} %add.87), channel_id=1, source_target_pairs={{0,64},{8,72},{16,80},{24,88},{32,40},{40,32},{48,56},{56,48},{64,... | collective-permute-start | bytes 589832 | tf_op jit(solution)/shard_map/ppermute | solution.py:381
  24.0 5.9 %collective-permute-done.15 = f32[4,128,256]{2,1,0:T(8,128)S(1)} collective-permute-done((f32[4,128,256]{2,1,0:T(8,128)S(1)}, f32[4,128,256]{2,1,0:T(8,128)S(1)}, u32[]{:S(2)}, u32[]{:S(2)}) %collective-permute-start.15) | collective-permute-done | bytes 524320 | tf_op jit(solution)/shard_map/ppermute | solution.py:381
  30.1 1.1 %collective-permute-start.14 = (f32[4,128,256]{2,1,0:T(8,128)S(1)}, f32[4,128,256]{2,1,0:T(8,128)S(1)}, u32[]{:S(2)}, u32[]{:S(2)}) collective-permute-start(f32[4,128,256]{2,1,0:T(8,128)S(1)} %get-tuple-element.28), channel_id=1, source_target_pairs={{0,192},{8,200},{16,208},{24,216},{32,56},{40,48},{48,40},{56,32},... | collective-permute-start | bytes 1572872 | tf_op jit(solution)/shard_map/ppermute | solution.py:381
  32.0 2.8 %collective-permute-start.2 = (f32[384,128]{1,0:T(8,128)S(1)}, f32[384,128]{1,0:T(8,128)S(1)}, u32[]{:S(2)}, u32[]{:S(2)}) collective-permute-start(f32[384,128]{1,0:T(8,128)S(1)} %add.88), channel_id=1, source_target_pairs={{0,192},{8,200},{16,208},{24,216},{32,56},{40,48},{48,40},{56,32},... | collective-permute-start | bytes 589832 | tf_op jit(solution)/shard_map/ppermute | solution.py:381
  34.9 6.9 %collective-permute-done.2 = f32[384,128]{1,0:T(8,128)S(1)} collective-permute-done((f32[384,128]{1,0:T(8,128)S(1)}, f32[384,128]{1,0:T(8,128)S(1)}, u32[]{:S(2)}, u32[]{:S(2)}) %collective-permute-start.2) | collective-permute-done | bytes 196640 | tf_op jit(solution)/shard_map/ppermute | solution.py:381
  43.8 1.8 %shard_map.66 = (f32[4,128,256]{2,1,0:T(8,128)S(1)}, f32[4,128,256]{2,1,0:T(8,128)S(1)}) custom-call(s32[32,1,1024]{2,1,0:T(1,128)S(1)} %get-tuple-element.19.heads_ref, s32[32,1,1024]{2,1,0:T(1,128)S(1)} %get-tuple-element.20.tails_ref, f32[32,1,1024]{2,1,0:T(1,128)S(1)} %get-tuple-element.21.values_ref, f32[8,256,128]{2,1,0:T(8,128)S(1)} %get-tuple-element.22.table_ref, ...), custom_call_target="tpu_custom_call" | custom-call | flops 536870912 | tf_op jit(solution)/shard_map/pallas_call | solution.py:160
  45.7 2.0 %collective-permute-start.17 = (f32[2,128,256]{2,1,0:T(8,128)S(1)}, f32[2,128,256]{2,1,0:T(8,128)S(1)}, u32[]{:S(2)}, u32[]{:S(2)}) collective-permute-start(f32[2,128,256]{2,1,0:T(8,128)S(1)} %slice_add_fusion), channel_id=1, source_target_pairs={{0,24},{8,16},{16,8},{24,0},{32,224},{40,232},{48,240},{56,248},{6... | collective-permute-start | bytes 786440 | tf_op jit(solution)/shard_map/ppermute | solution.py:381
  47.7 3.7 %collective-permute-done.11 = f32[4,128,256]{2,1,0:T(8,128)S(1)} collective-permute-done((f32[4,128,256]{2,1,0:T(8,128)S(1)}, f32[4,128,256]{2,1,0:T(8,128)S(1)}, u32[]{:S(2)}, u32[]{:S(2)}) %collective-permute-start.11) | collective-permute-done | bytes 524320 | tf_op jit(solution)/shard_map/ppermute | solution.py:381
  52.5 2.9 %collective-permute-done.17 = f32[2,128,256]{2,1,0:T(8,128)S(1)} collective-permute-done((f32[2,128,256]{2,1,0:T(8,128)S(1)}, f32[2,128,256]{2,1,0:T(8,128)S(1)}, u32[]{:S(2)}, u32[]{:S(2)}) %collective-permute-start.17) | collective-permute-done | bytes 262176 | tf_op jit(solution)/shard_map/ppermute | solution.py:381
  55.5 1.5 %collective-permute-done.12 = f32[2,128,256]{2,1,0:T(8,128)S(1)} collective-permute-done((f32[2,128,256]{2,1,0:T(8,128)S(1)}, f32[2,128,256]{2,1,0:T(8,128)S(1)}, u32[]{:S(2)}, u32[]{:S(2)}) %collective-permute-start.12) | collective-permute-done | bytes 262176 | tf_op jit(solution)/shard_map/ppermute | solution.py:381
  59.3 2.9 %collective-permute-done.13.ub_ref = f32[128,256]{1,0:T(8,128)S(1)} collective-permute-done((f32[128,256]{1,0:T(8,128)S(1)}, f32[128,256]{1,0:T(8,128)S(1)}, u32[]{:S(2)}, u32[]{:S(2)}) %collective-permute-start.13) | collective-permute-done | bytes 131104 | tf_op jit(solution)/shard_map/ppermute | solution.py:381
  62.2 6.3 %basis.1 = (f32[9,256,256]{2,1,0:T(8,128)S(1)}, f32[256,1,128]{2,1,0:T(1,128)S(1)}, f32[24,256]{1,0:T(8,128)S(1)}) custom-call(f32[384,128]{1,0:T(8,128)S(1)} %add.91.gram_ref, f32[128,256]{1,0:T(8,128)S(1)} %get-tuple-element.37.ua_ref, f32[128,256]{1,0:T(8,128)S(1)} %collective-permute-done.13.ub_ref, f32[128,256]{1,0:T(8,128)S(1)} %get-tuple-element.35.la_ref, ...), custom_call_target="tpu_custom_call" | custom-call | flops 2147483648 | tf_op jit(solution)/shard_map/basis/pallas_call | solution.py:263
  68.5 33.5 %all_to_all.5.inner_ref = f32[256,1,128]{2,1,0:T(1,128)S(1)} all-to-all(f32[256,1,128]{2,1,0:T(1,128)S(1)} %get-tuple-element.31), channel_id=1, replica_groups=mesh['ent_0'=4,'ent_1'=2,'blk'=4,'rel'=8] {'ent_0','ent_1','blk','rel'}, dimensions={0} | all-to-all | bytes 262144 | tf_op jit(solution)/shard_map/all_to_all | solution.py:438
  102.0 1.8 %solve.1 = (f32[1,256,256]{2,1,0:T(8,128)}, f32[1,256,256]{2,1,0:T(8,128)}) custom-call(f32[256,1,128]{2,1,0:T(1,128)S(1)} %all_to_all.5.inner_ref, f32[24,256]{1,0:T(8,128)S(1)} %get-tuple-element.32.coef_ref, f32[9,256,256]{2,1,0:T(8,128)S(1)} %get-tuple-element.33.basis_ref), custom_call_target="tpu_custom_call" | custom-call | tf_op jit(solution)/shard_map/solve/pallas_call | solution.py:354
  (37 shorter events, 10.0 us)
Async XLA Ops:
  4.0 5.6 %collective-permute-start.5 = (f32[4,256,256]{2,1,0:T(8,128)S(1)}, f32[4,256,256]{2,1,0:T(8,128)S(1)}, u32[]{:S(2)}, u32[]{:S(2)}) collective-permute-start(f32[4,256,256]{2,1,0:T(8,128)S(1)} %shard_map.59), channel_id=1, source_target_pairs={{0,32},{8,40},{16,48},{24,56},{32,0},{40,8},{48,16},{56,24},{64,96... | collective-permute-start | bytes 3145736 | tf_op jit(solution)/shard_map/ppermute | solution.py:381
  9.2 4.8 %collective-permute-start.6 = (f32[4,256,256]{2,1,0:T(8,128)S(1)}, f32[4,256,256]{2,1,0:T(8,128)S(1)}, u32[]{:S(2)}, u32[]{:S(2)}) collective-permute-start(f32[4,256,256]{2,1,0:T(8,128)S(1)} %shard_map.62), channel_id=1, source_target_pairs={{0,32},{8,40},{16,48},{24,56},{32,0},{40,8},{48,16},{56,24},{64,96... | collective-permute-start | bytes 3145736 | tf_op jit(solution)/shard_map/ppermute | solution.py:381
  13.3 2.9 %collective-permute-start.7 = (f32[4,256,256]{2,1,0:T(8,128)S(1)}, f32[4,256,256]{2,1,0:T(8,128)S(1)}, u32[]{:S(2)}, u32[]{:S(2)}) collective-permute-start(f32[4,256,256]{2,1,0:T(8,128)S(1)} %shard_map.61.rest_0_), channel_id=1, source_target_pairs={{0,32},{8,40},{16,48},{24,56},{32,0},{40,8},{48,16},{56,24},{64,96... | collective-permute-start | bytes 3145736 | tf_op jit(solution)/shard_map/ppermute | solution.py:381
  19.9 23.0 %collective-permute-start.8 = (f32[4,256,256]{2,1,0:T(8,128)S(1)}, f32[4,256,256]{2,1,0:T(8,128)S(1)}, u32[]{:S(2)}, u32[]{:S(2)}) collective-permute-start(f32[4,256,256]{2,1,0:T(8,128)S(1)} %shard_map.65), channel_id=1, source_target_pairs={{0,32},{8,40},{16,48},{24,56},{32,0},{40,8},{48,16},{56,24},{64,96... | collective-permute-start | bytes 3145736 | tf_op jit(solution)/shard_map/ppermute | solution.py:381
  20.4 9.5 %collective-permute-start.15 = (f32[4,128,256]{2,1,0:T(8,128)S(1)}, f32[4,128,256]{2,1,0:T(8,128)S(1)}, u32[]{:S(2)}, u32[]{:S(2)}) collective-permute-start(f32[4,128,256]{2,1,0:T(8,128)S(1)} %get-tuple-element.30), channel_id=1, source_target_pairs={{0,192},{8,200},{16,208},{24,216},{32,56},{40,48},{48,40},{56,32},... | collective-permute-start | bytes 1572872 | tf_op jit(solution)/shard_map/ppermute | solution.py:381
  21.4 1.5 %collective-permute-start = (f32[384,128]{1,0:T(8,128)S(1)}, f32[384,128]{1,0:T(8,128)S(1)}, u32[]{:S(2)}, u32[]{:S(2)}) collective-permute-start(f32[384,128]{1,0:T(8,128)S(1)} %get-tuple-element.18), channel_id=1, source_target_pairs={{0,32},{8,40},{16,48},{24,56},{32,0},{40,8},{48,16},{56,24},{64,96... | collective-permute-start | bytes 589832 | tf_op jit(solution)/shard_map/ppermute | solution.py:381
  21.6 13.3 %collective-permute-start.10 = (f32[4,128,256]{2,1,0:T(8,128)S(1)}, f32[4,128,256]{2,1,0:T(8,128)S(1)}, u32[]{:S(2)}, u32[]{:S(2)}) collective-permute-start(f32[4,128,256]{2,1,0:T(8,128)S(1)} %get-tuple-element.23.rest_0_), channel_id=1, source_target_pairs={{0,64},{8,72},{16,80},{24,88},{32,40},{40,32},{48,56},{56,48},{64,... | collective-permute-start | bytes 1572872 | tf_op jit(solution)/shard_map/ppermute | solution.py:381
  23.0 9.0 %collective-permute-start.1 = (f32[384,128]{1,0:T(8,128)S(1)}, f32[384,128]{1,0:T(8,128)S(1)}, u32[]{:S(2)}, u32[]{:S(2)}) collective-permute-start(f32[384,128]{1,0:T(8,128)S(1)} %add.87), channel_id=1, source_target_pairs={{0,64},{8,72},{16,80},{24,88},{32,40},{40,32},{48,56},{56,48},{64,... | collective-permute-start | bytes 589832 | tf_op jit(solution)/shard_map/ppermute | solution.py:381
  30.0 15.7 %collective-permute-start.16 = (f32[4,128,256]{2,1,0:T(8,128)S(1)}, f32[4,128,256]{2,1,0:T(8,128)S(1)}, u32[]{:S(2)}, u32[]{:S(2)}) collective-permute-start(f32[4,128,256]{2,1,0:T(8,128)S(1)} %add.104), channel_id=1, source_target_pairs={{0,64},{8,72},{16,80},{24,88},{32,40},{40,32},{48,56},{56,48},{64,... | collective-permute-start | bytes 1572872 | tf_op jit(solution)/shard_map/ppermute | solution.py:381
  30.1 15.6 %collective-permute-start.14 = (f32[4,128,256]{2,1,0:T(8,128)S(1)}, f32[4,128,256]{2,1,0:T(8,128)S(1)}, u32[]{:S(2)}, u32[]{:S(2)}) collective-permute-start(f32[4,128,256]{2,1,0:T(8,128)S(1)} %get-tuple-element.28), channel_id=1, source_target_pairs={{0,192},{8,200},{16,208},{24,216},{32,56},{40,48},{48,40},{56,32},... | collective-permute-start | bytes 1572872 | tf_op jit(solution)/shard_map/ppermute | solution.py:381
  32.0 9.8 %collective-permute-start.2 = (f32[384,128]{1,0:T(8,128)S(1)}, f32[384,128]{1,0:T(8,128)S(1)}, u32[]{:S(2)}, u32[]{:S(2)}) collective-permute-start(f32[384,128]{1,0:T(8,128)S(1)} %add.88), channel_id=1, source_target_pairs={{0,192},{8,200},{16,208},{24,216},{32,56},{40,48},{48,40},{56,32},... | collective-permute-start | bytes 589832 | tf_op jit(solution)/shard_map/ppermute | solution.py:381
  34.8 12.8 %collective-permute-start.9 = (f32[4,128,256]{2,1,0:T(8,128)S(1)}, f32[4,128,256]{2,1,0:T(8,128)S(1)}, u32[]{:S(2)}, u32[]{:S(2)}) collective-permute-start(f32[4,128,256]{2,1,0:T(8,128)S(1)} %get-tuple-element.24.rest_0_), channel_id=1, source_target_pairs={{0,64},{8,72},{16,80},{24,88},{32,40},{40,32},{48,56},{56,48},{64,... | collective-permute-start | bytes 1572872 | tf_op jit(solution)/shard_map/ppermute | solution.py:381
  41.8 9.5 %collective-permute-start.11 = (f32[4,128,256]{2,1,0:T(8,128)S(1)}, f32[4,128,256]{2,1,0:T(8,128)S(1)}, u32[]{:S(2)}, u32[]{:S(2)}) collective-permute-start(f32[4,128,256]{2,1,0:T(8,128)S(1)} %add.93), channel_id=1, source_target_pairs={{0,192},{8,200},{16,208},{24,216},{32,56},{40,48},{48,40},{56,32},... | collective-permute-start | bytes 1572872 | tf_op jit(solution)/shard_map/ppermute | solution.py:381
  42.9 8.6 %collective-permute-start.3 = (f32[384,128]{1,0:T(8,128)S(1)}, f32[384,128]{1,0:T(8,128)S(1)}, u32[]{:S(2)}, u32[]{:S(2)}) collective-permute-start(f32[384,128]{1,0:T(8,128)S(1)} %add.89), channel_id=1, source_target_pairs={{0,8},{8,0},{16,24},{24,16},{32,96},{40,104},{48,112},{56,120},{64... | collective-permute-start | bytes 589832 | tf_op jit(solution)/shard_map/ppermute | solution.py:381
  45.7 9.6 %collective-permute-start.17 = (f32[2,128,256]{2,1,0:T(8,128)S(1)}, f32[2,128,256]{2,1,0:T(8,128)S(1)}, u32[]{:S(2)}, u32[]{:S(2)}) collective-permute-start(f32[2,128,256]{2,1,0:T(8,128)S(1)} %slice_add_fusion), channel_id=1, source_target_pairs={{0,24},{8,16},{16,8},{24,0},{32,224},{40,232},{48,240},{56,248},{6... | collective-permute-start | bytes 786440 | tf_op jit(solution)/shard_map/ppermute | solution.py:381
  51.4 5.6 %collective-permute-start.12 = (f32[2,128,256]{2,1,0:T(8,128)S(1)}, f32[2,128,256]{2,1,0:T(8,128)S(1)}, u32[]{:S(2)}, u32[]{:S(2)}) collective-permute-start(f32[2,128,256]{2,1,0:T(8,128)S(1)} %slice_add_fusion.2), channel_id=1, source_target_pairs={{0,8},{8,0},{16,24},{24,16},{32,96},{40,104},{48,112},{56,120},{64... | collective-permute-start | bytes 786440 | tf_op jit(solution)/shard_map/ppermute | solution.py:381
  51.5 6.7 %collective-permute-start.4 = (f32[384,128]{1,0:T(8,128)S(1)}, f32[384,128]{1,0:T(8,128)S(1)}, u32[]{:S(2)}, u32[]{:S(2)}) collective-permute-start(f32[384,128]{1,0:T(8,128)S(1)} %add.90), channel_id=1, source_target_pairs={{0,24},{8,16},{16,8},{24,0},{32,224},{40,232},{48,240},{56,248},{6... | collective-permute-start | bytes 589832 | tf_op jit(solution)/shard_map/ppermute | solution.py:381
  55.4 3.9 %collective-permute-start.18 = (f32[128,256]{1,0:T(8,128)S(1)}, f32[128,256]{1,0:T(8,128)S(1)}, u32[]{:S(2)}, u32[]{:S(2)}) collective-permute-start(f32[128,256]{1,0:T(8,128)S(1)} %get-tuple-element.34), channel_id=1, source_target_pairs={{0,8},{8,0},{16,24},{24,16},{32,96},{40,104},{48,112},{56,120},{64... | collective-permute-start | bytes 393224 | tf_op jit(solution)/shard_map/ppermute | solution.py:381
  57.1 5.1 %collective-permute-start.13 = (f32[128,256]{1,0:T(8,128)S(1)}, f32[128,256]{1,0:T(8,128)S(1)}, u32[]{:S(2)}, u32[]{:S(2)}) collective-permute-start(f32[128,256]{1,0:T(8,128)S(1)} %get-tuple-element.36), channel_id=1, source_target_pairs={{0,24},{8,16},{16,8},{24,0},{32,224},{40,232},{48,240},{56,248},{6... | collective-permute-start | bytes 393224 | tf_op jit(solution)/shard_map/ppermute | solution.py:381
where the time goes:
time: 104 us
  blocking collectives  33.5 us (32%)
  waiting for transfers between devices  26.9 us (26%)
  Pallas kernels  24.3 us (23%)
  starting transfers between devices  17.8 us (17%)
    all_to_all x1, blocking collectives, fit(): inner = lax.all_to_all(inner, ENT_BLK_REL, 0, 0, tiled=True)  33.5 us
    ppermute x19, waiting for transfers between devices, shifted(): return lax.ppermute(array, axes, pairs)  26.9 us
    ppermute x19, starting transfers between devices, shifted(): return lax.ppermute(array, axes, pairs)  17.8 us
    pallas_call x8, Pallas kernels, triple_sums(): pl.pallas_call(functools.partial(triple_kernel, first=first, scale=scale,...  14.6 us
    pallas_call x1, Pallas kernels, basis_of(): pl.pallas_call(functools.partial(basis_kernel, ents=ents), out_shape=(plt...  6.34 us
  transfers between devices with their start and end apart: 19, of which 12 were waited for; matrix products, arithmetic and copies ran while one was open for 0% of the time, Pallas kernels for 9%

commit v1 on v0

--- a/solution.py
+++ b/solution.py
@@ -118,6 +118,22 @@
         inside = jnp.broadcast_to(ids_ref[relation, :, at] & (TILE - 1), (rank, TILE))
         return lane_pick(table_ref[block], inside).astype(BF16)
 
+    def rows_by_product(ids_ref, relation, tiles):
+        place = lax.broadcasted_iota(jnp.int32, (TILE, TILE), 0)
+        nothing = jnp.zeros((TILE, TILE), BF16)
+        blocks, picks = [], []
+        for tile in tiles:
+            at = slice(tile * TILE, (tile + 1) * TILE)
+            block = ids_ref[relation, 0, tile * TILE] // TILE
+            inside = ids_ref[relation, :, at] & (TILE - 1)
+            blocks.append(table_ref[block].astype(BF16))
+            picks.append(jnp.where(place == inside, 1.0, 0.0).astype(BF16))
+        pick = jnp.concatenate(
+            [jnp.concatenate([picks[0], nothing], axis=1), jnp.concatenate([nothing, picks[1]], axis=1)], axis=0
+        )
+        return dot(jnp.concatenate(blocks, axis=1), pick).astype(BF16)
+
+    by_product = (0, 6)
     for i in range(columns):
         to_x = x ^ jnp.where(to_core == 0, first, i)
         to_y = y ^ jnp.where(to_core == 0, i, first)
@@ -131,7 +147,10 @@
                 head_rows = rows(heads_ref, relation, tile).astype(F32)
                 weighted.append((head_rows * values_ref[relation, :, at]).astype(BF16))
             weighted = jnp.concatenate(weighted, axis=1)
-            tail_rows = jnp.concatenate([rows(tails_ref, relation, tile) for tile in tiles], axis=1)
+            if pair in by_product and len(tiles) == 2:
+                tail_rows = rows_by_product(tails_ref, relation, tiles)
+            else:
+                tail_rows = jnp.concatenate([rows(tails_ref, relation, tile) for tile in tiles], axis=1)
             part = lax.dot_general(
                 weighted, tail_rows, (((1,), (1,)), ((), ())), preferred_element_type=F32
             )

time: 104 us -> 103 us (level)
  Pallas kernels: 24.3 us -> 22.5 us
    pallas_call x8, Pallas kernels: 14.6 us -> 12.7 us  [triple_sums(): pl.pallas_call(functools.partial(triple_kernel, first=first, scale=scale,...]
  transfers between devices with their start and end apart: 19 -> 19, of which waited for: 12 -> 12; matrix products, arithmetic and copies ran while one was open for 0% -> 0% of each run, Pallas kernels for 9% -> 8%
where the time goes in v1:
time: 103 us; the launch traced here: 102 us
  blocking collectives  33.3 us (32%)
  waiting for transfers between devices  27.6 us (27%)
  Pallas kernels  22.5 us (22%)
  starting transfers between devices  17.8 us (17%)
    all_to_all x1, blocking collectives, fit(): inner = lax.all_to_all(inner, ENT_BLK_REL, 0, 0, tiled=True)  33.3 us
    ppermute x19, waiting for transfers between devices, shifted(): return lax.ppermute(array, axes, pairs)  27.6 us
    ppermute x19, starting transfers between devices, shifted(): return lax.ppermute(array, axes, pairs)  17.8 us
    pallas_call x8, Pallas kernels, triple_sums(): pl.pallas_call(functools.partial(triple_kernel, first=first, scale=scale,...  12.7 us
    pallas_call x1, Pallas kernels, basis_of(): pl.pallas_call(functools.partial(basis_kernel, ents=ents), out_shape=(plt...  6.34 us
  transfers between devices with their start and end apart: 19, of which 12 were waited for; matrix products, arithmetic and copies ran while one was open for 0% of the time, Pallas kernels for 8%

profile of v1, /device:TPU:1, one launch (start us, length us, event | category | flops | bytes accessed | tf_op | source)
XLA Modules:
  0.0 102.5 jit_solution(12611818581290917941)
XLA Ops:
  0.6 1.6 %tables.1 = (f32[8,256,128]{2,1,0:T(8,128)S(1)}, f32[384,128]{1,0:T(8,128)S(1)}, s32[32,1,1024]{2,1,0:T(1,128)S(1)}, s32[32,1,1024]{2,1,0:T(1,128)S(1)}, f32[32,1,1024]{2,1,0:T(1,128)S(1)}) custom-call(bf16[1024,256]{1,0:T(8,128)(2,1)} %factors_hbm.1, s32[32,1,1024]{2,1,0:T(1,128)} %bitcast.11, s32[32,1,1024]{2,1,0:T(1,128)} %bitcast.12, f32[32,1,1024]{2,1,0:T(1,128)} %bitcast.13), custom_call_target="tpu_custom_call" | custom-call | tf_op jit(solution)/shard_map/tables/pallas_call | solution.py:66
  2.2 1.6 %shard_map.59 = f32[4,256,256]{2,1,0:T(8,128)S(1)} custom-call(s32[32,1,1024]{2,1,0:T(1,128)S(1)} %get-tuple-element.19.heads_ref, s32[32,1,1024]{2,1,0:T(1,128)S(1)} %get-tuple-element.20.tails_ref, f32[32,1,1024]{2,1,0:T(1,128)S(1)} %get-tuple-element.21.values_ref, f32[8,256,128]{2,1,0:T(8,128)S(1)} %get-tuple-element.22.table_ref), custom_call_target="tpu_custom_call" | custom-call | flops 536870912 | tf_op jit(solution)/shard_map/pallas_call | solution.py:179
  3.8 3.3 %collective-permute-start.5 = (f32[4,256,256]{2,1,0:T(8,128)S(1)}, f32[4,256,256]{2,1,0:T(8,128)S(1)}, u32[]{:S(2)}, u32[]{:S(2)}) collective-permute-start(f32[4,256,256]{2,1,0:T(8,128)S(1)} %shard_map.59), channel_id=1, source_target_pairs={{0,32},{8,40},{16,48},{24,56},{32,0},{40,8},{48,16},{56,24},{64,96... | collective-permute-start | bytes 3145736 | tf_op jit(solution)/shard_map/ppermute | solution.py:400
  7.1 1.6 %shard_map.62 = f32[4,256,256]{2,1,0:T(8,128)S(1)} custom-call(s32[32,1,1024]{2,1,0:T(1,128)S(1)} %get-tuple-element.19.heads_ref, s32[32,1,1024]{2,1,0:T(1,128)S(1)} %get-tuple-element.20.tails_ref, f32[32,1,1024]{2,1,0:T(1,128)S(1)} %get-tuple-element.21.values_ref, f32[8,256,128]{2,1,0:T(8,128)S(1)} %get-tuple-element.22.table_ref), custom_call_target="tpu_custom_call" | custom-call | flops 536870912 | tf_op jit(solution)/shard_map/pallas_call | solution.py:179
  9.4 1.6 %shard_map.60 = (f32[4,128,256]{2,1,0:T(8,128)S(1)}, f32[4,128,256]{2,1,0:T(8,128)S(1)}) custom-call(s32[32,1,1024]{2,1,0:T(1,128)S(1)} %get-tuple-element.19.heads_ref, s32[32,1,1024]{2,1,0:T(1,128)S(1)} %get-tuple-element.20.tails_ref, f32[32,1,1024]{2,1,0:T(1,128)S(1)} %get-tuple-element.21.values_ref, f32[8,256,128]{2,1,0:T(8,128)S(1)} %get-tuple-element.22.table_ref, ...), custom_call_target="tpu_custom_call" | custom-call | flops 536870912 | tf_op jit(solution)/shard_map/pallas_call | solution.py:179
  11.0 1.6 %shard_map.61.rest_0_ = f32[4,256,256]{2,1,0:T(8,128)S(1)} custom-call(s32[32,1,1024]{2,1,0:T(1,128)S(1)} %get-tuple-element.19.heads_ref, s32[32,1,1024]{2,1,0:T(1,128)S(1)} %get-tuple-element.20.tails_ref, f32[32,1,1024]{2,1,0:T(1,128)S(1)} %get-tuple-element.21.values_ref, f32[8,256,128]{2,1,0:T(8,128)S(1)} %get-tuple-element.22.table_ref, ...), custom_call_target="tpu_custom_call" | custom-call | flops 536870912 | tf_op jit(solution)/shard_map/pallas_call | solution.py:179
  13.2 1.6 %shard_map.63 = (f32[4,128,256]{2,1,0:T(8,128)S(1)}, f32[4,128,256]{2,1,0:T(8,128)S(1)}) custom-call(s32[32,1,1024]{2,1,0:T(1,128)S(1)} %get-tuple-element.19.heads_ref, s32[32,1,1024]{2,1,0:T(1,128)S(1)} %get-tuple-element.20.tails_ref, f32[32,1,1024]{2,1,0:T(1,128)S(1)} %get-tuple-element.21.values_ref, f32[8,256,128]{2,1,0:T(8,128)S(1)} %get-tuple-element.22.table_ref, ...), custom_call_target="tpu_custom_call" | custom-call | flops 536870912 | tf_op jit(solution)/shard_map/pallas_call | solution.py:179
  15.5 1.6 %shard_map.64 = (f32[4,128,256]{2,1,0:T(8,128)S(1)}, f32[4,128,256]{2,1,0:T(8,128)S(1)}) custom-call(s32[32,1,1024]{2,1,0:T(1,128)S(1)} %get-tuple-element.19.heads_ref, s32[32,1,1024]{2,1,0:T(1,128)S(1)} %get-tuple-element.20.tails_ref, f32[32,1,1024]{2,1,0:T(1,128)S(1)} %get-tuple-element.21.values_ref, f32[8,256,128]{2,1,0:T(8,128)S(1)} %get-tuple-element.22.table_ref, ...), custom_call_target="tpu_custom_call" | custom-call | flops 536870912 | tf_op jit(solution)/shard_map/pallas_call | solution.py:179
  17.1 1.6 %shard_map.65 = f32[4,256,256]{2,1,0:T(8,128)S(1)} custom-call(s32[32,1,1024]{2,1,0:T(1,128)S(1)} %get-tuple-element.19.heads_ref, s32[32,1,1024]{2,1,0:T(1,128)S(1)} %get-tuple-element.20.tails_ref, f32[32,1,1024]{2,1,0:T(1,128)S(1)} %get-tuple-element.21.values_ref, f32[8,256,128]{2,1,0:T(8,128)S(1)} %get-tuple-element.22.table_ref, ...), custom_call_target="tpu_custom_call" | custom-call | flops 536870912 | tf_op jit(solution)/shard_map/pallas_call | solution.py:179
  20.4 1.3 %collective-permute-start.10 = (f32[4,128,256]{2,1,0:T(8,128)S(1)}, f32[4,128,256]{2,1,0:T(8,128)S(1)}, u32[]{:S(2)}, u32[]{:S(2)}) collective-permute-start(f32[4,128,256]{2,1,0:T(8,128)S(1)} %get-tuple-element.23.rest_0_), channel_id=1, source_target_pairs={{0,64},{8,72},{16,80},{24,88},{32,40},{40,32},{48,56},{56,48},{64,... | collective-permute-start | bytes 1572872 | tf_op jit(solution)/shard_map/ppermute | solution.py:400
  21.8 1.1 %collective-permute-start.1 = (f32[384,128]{1,0:T(8,128)S(1)}, f32[384,128]{1,0:T(8,128)S(1)}, u32[]{:S(2)}, u32[]{:S(2)}) collective-permute-start(f32[384,128]{1,0:T(8,128)S(1)} %add.87), channel_id=1, source_target_pairs={{0,64},{8,72},{16,80},{24,88},{32,40},{40,32},{48,56},{56,48},{64,... | collective-permute-start | bytes 589832 | tf_op jit(solution)/shard_map/ppermute | solution.py:400
  22.9 5.9 %collective-permute-done.15 = f32[4,128,256]{2,1,0:T(8,128)S(1)} collective-permute-done((f32[4,128,256]{2,1,0:T(8,128)S(1)}, f32[4,128,256]{2,1,0:T(8,128)S(1)}, u32[]{:S(2)}, u32[]{:S(2)}) %collective-permute-start.15) | collective-permute-done | bytes 524320 | tf_op jit(solution)/shard_map/ppermute | solution.py:400
  28.9 1.1 %collective-permute-start.14 = (f32[4,128,256]{2,1,0:T(8,128)S(1)}, f32[4,128,256]{2,1,0:T(8,128)S(1)}, u32[]{:S(2)}, u32[]{:S(2)}) collective-permute-start(f32[4,128,256]{2,1,0:T(8,128)S(1)} %get-tuple-element.28), channel_id=1, source_target_pairs={{0,192},{8,200},{16,208},{24,216},{32,56},{40,48},{48,40},{56,32},... | collective-permute-start | bytes 1572872 | tf_op jit(solution)/shard_map/ppermute | solution.py:400
  30.8 2.8 %collective-permute-start.2 = (f32[384,128]{1,0:T(8,128)S(1)}, f32[384,128]{1,0:T(8,128)S(1)}, u32[]{:S(2)}, u32[]{:S(2)}) collective-permute-start(f32[384,128]{1,0:T(8,128)S(1)} %add.88), channel_id=1, source_target_pairs={{0,192},{8,200},{16,208},{24,216},{32,56},{40,48},{48,40},{56,32},... | collective-permute-start | bytes 589832 | tf_op jit(solution)/shard_map/ppermute | solution.py:400
  33.7 6.9 %collective-permute-done.2 = f32[384,128]{1,0:T(8,128)S(1)} collective-permute-done((f32[384,128]{1,0:T(8,128)S(1)}, f32[384,128]{1,0:T(8,128)S(1)}, u32[]{:S(2)}, u32[]{:S(2)}) %collective-permute-start.2) | collective-permute-done | bytes 196640 | tf_op jit(solution)/shard_map/ppermute | solution.py:400
  42.4 1.6 %shard_map.66 = (f32[4,128,256]{2,1,0:T(8,128)S(1)}, f32[4,128,256]{2,1,0:T(8,128)S(1)}) custom-call(s32[32,1,1024]{2,1,0:T(1,128)S(1)} %get-tuple-element.19.heads_ref, s32[32,1,1024]{2,1,0:T(1,128)S(1)} %get-tuple-element.20.tails_ref, f32[32,1,1024]{2,1,0:T(1,128)S(1)} %get-tuple-element.21.values_ref, f32[8,256,128]{2,1,0:T(8,128)S(1)} %get-tuple-element.22.table_ref, ...), custom_call_target="tpu_custom_call" | custom-call | flops 536870912 | tf_op jit(solution)/shard_map/pallas_call | solution.py:179
  44.1 2.2 %collective-permute-start.17 = (f32[2,128,256]{2,1,0:T(8,128)S(1)}, f32[2,128,256]{2,1,0:T(8,128)S(1)}, u32[]{:S(2)}, u32[]{:S(2)}) collective-permute-start(f32[2,128,256]{2,1,0:T(8,128)S(1)} %slice_add_fusion), channel_id=1, source_target_pairs={{0,24},{8,16},{16,8},{24,0},{32,224},{40,232},{48,240},{56,248},{6... | collective-permute-start | bytes 786440 | tf_op jit(solution)/shard_map/ppermute | solution.py:400
  46.3 3.9 %collective-permute-done.11 = f32[4,128,256]{2,1,0:T(8,128)S(1)} collective-permute-done((f32[4,128,256]{2,1,0:T(8,128)S(1)}, f32[4,128,256]{2,1,0:T(8,128)S(1)}, u32[]{:S(2)}, u32[]{:S(2)}) %collective-permute-start.11) | collective-permute-done | bytes 524320 | tf_op jit(solution)/shard_map/ppermute | solution.py:400
  51.3 2.6 %collective-permute-done.17 = f32[2,128,256]{2,1,0:T(8,128)S(1)} collective-permute-done((f32[2,128,256]{2,1,0:T(8,128)S(1)}, f32[2,128,256]{2,1,0:T(8,128)S(1)}, u32[]{:S(2)}, u32[]{:S(2)}) %collective-permute-start.17) | collective-permute-done | bytes 262176 | tf_op jit(solution)/shard_map/ppermute | solution.py:400
  54.1 1.7 %collective-permute-done.12 = f32[2,128,256]{2,1,0:T(8,128)S(1)} collective-permute-done((f32[2,128,256]{2,1,0:T(8,128)S(1)}, f32[2,128,256]{2,1,0:T(8,128)S(1)}, u32[]{:S(2)}, u32[]{:S(2)}) %collective-permute-start.12) | collective-permute-done | bytes 262176 | tf_op jit(solution)/shard_map/ppermute | solution.py:400
  57.9 3.1 %collective-permute-done.13.ub_ref = f32[128,256]{1,0:T(8,128)S(1)} collective-permute-done((f32[128,256]{1,0:T(8,128)S(1)}, f32[128,256]{1,0:T(8,128)S(1)}, u32[]{:S(2)}, u32[]{:S(2)}) %collective-permute-start.13) | collective-permute-done | bytes 131104 | tf_op jit(solution)/shard_map/ppermute | solution.py:400
  61.0 6.3 %basis.1 = (f32[9,256,256]{2,1,0:T(8,128)S(1)}, f32[256,1,128]{2,1,0:T(1,128)S(1)}, f32[24,256]{1,0:T(8,128)S(1)}) custom-call(f32[384,128]{1,0:T(8,128)S(1)} %add.91.gram_ref, f32[128,256]{1,0:T(8,128)S(1)} %get-tuple-element.37.ua_ref, f32[128,256]{1,0:T(8,128)S(1)} %collective-permute-done.13.ub_ref, f32[128,256]{1,0:T(8,128)S(1)} %get-tuple-element.35.la_ref, ...), custom_call_target="tpu_custom_call" | custom-call | flops 2147483648 | tf_op jit(solution)/shard_map/basis/pallas_call | solution.py:282
  67.3 33.3 %all_to_all.5.inner_ref = f32[256,1,128]{2,1,0:T(1,128)S(1)} all-to-all(f32[256,1,128]{2,1,0:T(1,128)S(1)} %get-tuple-element.31), channel_id=1, replica_groups=mesh['ent_0'=4,'ent_1'=2,'blk'=4,'rel'=8] {'ent_0','ent_1','blk','rel'}, dimensions={0} | all-to-all | bytes 262144 | tf_op jit(solution)/shard_map/all_to_all | solution.py:457
  100.6 1.8 %solve.1 = (f32[1,256,256]{2,1,0:T(8,128)}, f32[1,256,256]{2,1,0:T(8,128)}) custom-call(f32[256,1,128]{2,1,0:T(1,128)S(1)} %all_to_all.5.inner_ref, f32[24,256]{1,0:T(8,128)S(1)} %get-tuple-element.32.coef_ref, f32[9,256,256]{2,1,0:T(8,128)S(1)} %get-tuple-element.33.basis_ref), custom_call_target="tpu_custom_call" | custom-call | tf_op jit(solution)/shard_map/solve/pallas_call | solution.py:373
  (37 shorter events, 10.0 us)
Async XLA Ops:
  3.8 5.6 %collective-permute-start.5 = (f32[4,256,256]{2,1,0:T(8,128)S(1)}, f32[4,256,256]{2,1,0:T(8,128)S(1)}, u32[]{:S(2)}, u32[]{:S(2)}) collective-permute-start(f32[4,256,256]{2,1,0:T(8,128)S(1)} %shard_map.59), channel_id=1, source_target_pairs={{0,32},{8,40},{16,48},{24,56},{32,0},{40,8},{48,16},{56,24},{64,96... | collective-permute-start | bytes 3145736 | tf_op jit(solution)/shard_map/ppermute | solution.py:400
  8.7 4.5 %collective-permute-start.6 = (f32[4,256,256]{2,1,0:T(8,128)S(1)}, f32[4,256,256]{2,1,0:T(8,128)S(1)}, u32[]{:S(2)}, u32[]{:S(2)}) collective-permute-start(f32[4,256,256]{2,1,0:T(8,128)S(1)} %shard_map.62), channel_id=1, source_target_pairs={{0,32},{8,40},{16,48},{24,56},{32,0},{40,8},{48,16},{56,24},{64,96... | collective-permute-start | bytes 3145736 | tf_op jit(solution)/shard_map/ppermute | solution.py:400
  12.6 2.9 %collective-permute-start.7 = (f32[4,256,256]{2,1,0:T(8,128)S(1)}, f32[4,256,256]{2,1,0:T(8,128)S(1)}, u32[]{:S(2)}, u32[]{:S(2)}) collective-permute-start(f32[4,256,256]{2,1,0:T(8,128)S(1)} %shard_map.61.rest_0_), channel_id=1, source_target_pairs={{0,32},{8,40},{16,48},{24,56},{32,0},{40,8},{48,16},{56,24},{64,96... | collective-permute-start | bytes 3145736 | tf_op jit(solution)/shard_map/ppermute | solution.py:400
  18.7 23.0 %collective-permute-start.8 = (f32[4,256,256]{2,1,0:T(8,128)S(1)}, f32[4,256,256]{2,1,0:T(8,128)S(1)}, u32[]{:S(2)}, u32[]{:S(2)}) collective-permute-start(f32[4,256,256]{2,1,0:T(8,128)S(1)} %shard_map.65), channel_id=1, source_target_pairs={{0,32},{8,40},{16,48},{24,56},{32,0},{40,8},{48,16},{56,24},{64,96... | collective-permute-start | bytes 3145736 | tf_op jit(solution)/shard_map/ppermute | solution.py:400
  19.2 9.5 %collective-permute-start.15 = (f32[4,128,256]{2,1,0:T(8,128)S(1)}, f32[4,128,256]{2,1,0:T(8,128)S(1)}, u32[]{:S(2)}, u32[]{:S(2)}) collective-permute-start(f32[4,128,256]{2,1,0:T(8,128)S(1)} %get-tuple-element.30), channel_id=1, source_target_pairs={{0,192},{8,200},{16,208},{24,216},{32,56},{40,48},{48,40},{56,32},... | collective-permute-start | bytes 1572872 | tf_op jit(solution)/shard_map/ppermute | solution.py:400
  20.2 1.5 %collective-permute-start = (f32[384,128]{1,0:T(8,128)S(1)}, f32[384,128]{1,0:T(8,128)S(1)}, u32[]{:S(2)}, u32[]{:S(2)}) collective-permute-start(f32[384,128]{1,0:T(8,128)S(1)} %get-tuple-element.18), channel_id=1, source_target_pairs={{0,32},{8,40},{16,48},{24,56},{32,0},{40,8},{48,16},{56,24},{64,96... | collective-permute-start | bytes 589832 | tf_op jit(solution)/shard_map/ppermute | solution.py:400
  20.4 13.3 %collective-permute-start.10 = (f32[4,128,256]{2,1,0:T(8,128)S(1)}, f32[4,128,256]{2,1,0:T(8,128)S(1)}, u32[]{:S(2)}, u32[]{:S(2)}) collective-permute-start(f32[4,128,256]{2,1,0:T(8,128)S(1)} %get-tuple-element.23.rest_0_), channel_id=1, source_target_pairs={{0,64},{8,72},{16,80},{24,88},{32,40},{40,32},{48,56},{56,48},{64,... | collective-permute-start | bytes 1572872 | tf_op jit(solution)/shard_map/ppermute | solution.py:400
  21.8 9.0 %collective-permute-start.1 = (f32[384,128]{1,0:T(8,128)S(1)}, f32[384,128]{1,0:T(8,128)S(1)}, u32[]{:S(2)}, u32[]{:S(2)}) collective-permute-start(f32[384,128]{1,0:T(8,128)S(1)} %add.87), channel_id=1, source_target_pairs={{0,64},{8,72},{16,80},{24,88},{32,40},{40,32},{48,56},{56,48},{64,... | collective-permute-start | bytes 589832 | tf_op jit(solution)/shard_map/ppermute | solution.py:400
  28.8 15.2 %collective-permute-start.16 = (f32[4,128,256]{2,1,0:T(8,128)S(1)}, f32[4,128,256]{2,1,0:T(8,128)S(1)}, u32[]{:S(2)}, u32[]{:S(2)}) collective-permute-start(f32[4,128,256]{2,1,0:T(8,128)S(1)} %add.104), channel_id=1, source_target_pairs={{0,64},{8,72},{16,80},{24,88},{32,40},{40,32},{48,56},{56,48},{64,... | collective-permute-start | bytes 1572872 | tf_op jit(solution)/shard_map/ppermute | solution.py:400
  28.9 15.1 %collective-permute-start.14 = (f32[4,128,256]{2,1,0:T(8,128)S(1)}, f32[4,128,256]{2,1,0:T(8,128)S(1)}, u32[]{:S(2)}, u32[]{:S(2)}) collective-permute-start(f32[4,128,256]{2,1,0:T(8,128)S(1)} %get-tuple-element.28), channel_id=1, source_target_pairs={{0,192},{8,200},{16,208},{24,216},{32,56},{40,48},{48,40},{56,32},... | collective-permute-start | bytes 1572872 | tf_op jit(solution)/shard_map/ppermute | solution.py:400
  30.8 9.8 %collective-permute-start.2 = (f32[384,128]{1,0:T(8,128)S(1)}, f32[384,128]{1,0:T(8,128)S(1)}, u32[]{:S(2)}, u32[]{:S(2)}) collective-permute-start(f32[384,128]{1,0:T(8,128)S(1)} %add.88), channel_id=1, source_target_pairs={{0,192},{8,200},{16,208},{24,216},{32,56},{40,48},{48,40},{56,32},... | collective-permute-start | bytes 589832 | tf_op jit(solution)/shard_map/ppermute | solution.py:400
  33.6 12.6 %collective-permute-start.9 = (f32[4,128,256]{2,1,0:T(8,128)S(1)}, f32[4,128,256]{2,1,0:T(8,128)S(1)}, u32[]{:S(2)}, u32[]{:S(2)}) collective-permute-start(f32[4,128,256]{2,1,0:T(8,128)S(1)} %get-tuple-element.24.rest_0_), channel_id=1, source_target_pairs={{0,64},{8,72},{16,80},{24,88},{32,40},{40,32},{48,56},{56,48},{64,... | collective-permute-start | bytes 1572872 | tf_op jit(solution)/shard_map/ppermute | solution.py:400
  40.6 9.5 %collective-permute-start.11 = (f32[4,128,256]{2,1,0:T(8,128)S(1)}, f32[4,128,256]{2,1,0:T(8,128)S(1)}, u32[]{:S(2)}, u32[]{:S(2)}) collective-permute-start(f32[4,128,256]{2,1,0:T(8,128)S(1)} %add.93), channel_id=1, source_target_pairs={{0,192},{8,200},{16,208},{24,216},{32,56},{40,48},{48,40},{56,32},... | collective-permute-start | bytes 1572872 | tf_op jit(solution)/shard_map/ppermute | solution.py:400
  41.7 8.6 %collective-permute-start.3 = (f32[384,128]{1,0:T(8,128)S(1)}, f32[384,128]{1,0:T(8,128)S(1)}, u32[]{:S(2)}, u32[]{:S(2)}) collective-permute-start(f32[384,128]{1,0:T(8,128)S(1)} %add.89), channel_id=1, source_target_pairs={{0,8},{8,0},{16,24},{24,16},{32,96},{40,104},{48,112},{56,120},{64... | collective-permute-start | bytes 589832 | tf_op jit(solution)/shard_map/ppermute | solution.py:400
  44.1 9.8 %collective-permute-start.17 = (f32[2,128,256]{2,1,0:T(8,128)S(1)}, f32[2,128,256]{2,1,0:T(8,128)S(1)}, u32[]{:S(2)}, u32[]{:S(2)}) collective-permute-start(f32[2,128,256]{2,1,0:T(8,128)S(1)} %slice_add_fusion), channel_id=1, source_target_pairs={{0,24},{8,16},{16,8},{24,0},{32,224},{40,232},{48,240},{56,248},{6... | collective-permute-start | bytes 786440 | tf_op jit(solution)/shard_map/ppermute | solution.py:400
  50.2 5.6 %collective-permute-start.12 = (f32[2,128,256]{2,1,0:T(8,128)S(1)}, f32[2,128,256]{2,1,0:T(8,128)S(1)}, u32[]{:S(2)}, u32[]{:S(2)}) collective-permute-start(f32[2,128,256]{2,1,0:T(8,128)S(1)} %slice_add_fusion.2), channel_id=1, source_target_pairs={{0,8},{8,0},{16,24},{24,16},{32,96},{40,104},{48,112},{56,120},{64... | collective-permute-start | bytes 786440 | tf_op jit(solution)/shard_map/ppermute | solution.py:400
  50.3 6.7 %collective-permute-start.4 = (f32[384,128]{1,0:T(8,128)S(1)}, f32[384,128]{1,0:T(8,128)S(1)}, u32[]{:S(2)}, u32[]{:S(2)}) collective-permute-start(f32[384,128]{1,0:T(8,128)S(1)} %add.90), channel_id=1, source_target_pairs={{0,24},{8,16},{16,8},{24,0},{32,224},{40,232},{48,240},{56,248},{6... | collective-permute-start | bytes 589832 | tf_op jit(solution)/shard_map/ppermute | solution.py:400
  54.0 3.9 %collective-permute-start.18 = (f32[128,256]{1,0:T(8,128)S(1)}, f32[128,256]{1,0:T(8,128)S(1)}, u32[]{:S(2)}, u32[]{:S(2)}) collective-permute-start(f32[128,256]{1,0:T(8,128)S(1)} %get-tuple-element.34), channel_id=1, source_target_pairs={{0,8},{8,0},{16,24},{24,16},{32,96},{40,104},{48,112},{56,120},{64... | collective-permute-start | bytes 393224 | tf_op jit(solution)/shard_map/ppermute | solution.py:400
  55.9 5.1 %collective-permute-start.13 = (f32[128,256]{1,0:T(8,128)S(1)}, f32[128,256]{1,0:T(8,128)S(1)}, u32[]{:S(2)}, u32[]{:S(2)}) collective-permute-start(f32[128,256]{1,0:T(8,128)S(1)} %get-tuple-element.36), channel_id=1, source_target_pairs={{0,24},{8,16},{16,8},{24,0},{32,224},{40,232},{48,240},{56,248},{6... | collective-permute-start | bytes 393224 | tf_op jit(solution)/shard_map/ppermute | solution.py:400
